TPU v7x, 256 devices: a 4x2x16 block of a 4x16x16 slice. The times are simulated.
256 devices in a mesh: grp: 2 (over y), sub: 128 (over z, x, core).
Axes of the slice: x: 4, y: 2, z: 16, core: 2. Of those that a mesh axis runs over, the one named last changes fastest.
The devices are a block of a 4x16x16 slice.
Arguments:
- factors: bfloat16 [768, 1024, 1024], P(('grp', 'sub')), parts along dimension 0, may hold values from -0.1875 to 0.1875
- coupling: bfloat16 [768, 1024, 512], P(('grp', 'sub')), parts along dimension 0, may hold values from -0.1875 to 0.1875
- gap_loads: bfloat16 [768, 512, 256], P(('grp', 'sub')), parts along dimension 0, may hold values from -6 to 6
- dof_blocks: int32 [768], P(('grp', 'sub')), parts along dimension 0, may hold values from 4 to 8, as said below
- partner_rows: int32 [768, 512], P(('grp', 'sub')), parts along dimension 0, may hold values from 0 to 196607, as said below
Outputs:
- multipliers: float32 [768, 512, 256], P(('grp', 'sub')), parts along dimension 0
- dual_residual: float32 [768, 512, 256], P(('grp', 'sub')), parts along dimension 0
- residual_rms: float32 [512], P('grp'), parts along dimension 0
There are 2 independent parts, one for each index of `grp`. A program takes and returns all parts, laid end to end along the dimension named above; each array names one. Nothing has to cross between parts.
Inputs may be any that keep to these rules, and one draw needn't show every extreme that they name: `partner_rows`: every interface row is tied to exactly one row of a subdomain on another device, and that row is tied back to it. The rows of one device are tied to at most 16 rows of any one other device, and some pair of devices reaches that number in every draw. `dof_blocks`: some subdomain has all 1024 degrees of freedom present in every draw.
All inputs are finite; a program needn't handle non-finite values.
Results may differ from a plain program's by a relative error of at most 0.008.
Values may be sent and summed in bfloat16 or wider, within the bound.
No kernel may reach another device: no remote copies, remote signals or barrier semaphores. Data moves between devices by JAX's collectives and lax.ppermute only.
A program may use at most 64 MiB of HBM per device.

v0:
```python
import functools

import jax
import jax.numpy as jnp
from jax import lax
from jax.sharding import Mesh
from jax.sharding import PartitionSpec as P

DBLK = 128
FROWS = 16
ITERS = 3
SUB = ("sub_0", "sub_1", "sub_2")
GRP_SUB = ("grp", "sub_0", "sub_1", "sub_2")


STEP_SIZE = 0.25


def by_axis(value, axes):
    return functools.reduce(lax.psum, axes, value)


def masked_coupling(couple, blocks):
    present = jnp.arange(couple.shape[0]) < blocks * DBLK
    return (jnp.where(present[:, None], couple, jnp.zeros_like(couple)), present)


def whole_panel(factor, couple, blocks):
    masked, present = masked_coupling(couple, blocks)
    product = lax.dot_general(
        factor, masked, (((0,), (0,)), ((), ())), preferred_element_type=jnp.float32
    )
    reduced = jnp.where(present[:, None], product, jnp.zeros_like(product)).astype(jnp.bfloat16)
    schur_panel = lax.dot_general(
        reduced, reduced, (((0,), (0,)), ((), ())), preferred_element_type=jnp.float32
    )
    return schur_panel.astype(jnp.bfloat16)


def local(factors, coupling, gap_loads, dof_blocks, partner_rows):
    subdomains, interface, load_cases = gap_loads.shape
    devices = lax.axis_size(SUB)
    position = lax.axis_index(SUB)
    row_count = subdomains * interface
    partners = partner_rows.reshape(row_count)
    own_rows = position * row_count + jnp.arange(row_count, dtype=jnp.int32)
    orient = (
        jnp.where(own_rows < partners, 1.0, -1.0)
        .astype(jnp.float32)
        .reshape(subdomains, interface, 1)
    )
    target = partners // row_count
    remote = partners - target * row_count
    same_peer = target[:, None] == target[None, :]
    ordinal = jnp.arange(row_count, dtype=jnp.int32)
    send_slot = jnp.sum(same_peer & (ordinal[None, :] < ordinal[:, None]), axis=1, dtype=jnp.int32)
    read_slot = jnp.sum(same_peer & (remote[None, :] < remote[:, None]), axis=1, dtype=jnp.int32)
    spread = max(devices // 2 - 1, 1)
    capacity = FROWS * ((row_count // FROWS // 2 + spread - 1) // spread)

    def outgoing_of(values, kind):
        flat_values = values.reshape(row_count, values.shape[2])
        buffer = jnp.zeros((devices, capacity, values.shape[2]), kind)
        return (flat_values, buffer.at[target, send_slot].set(flat_values))

    def combine_rows(flat_values, incoming, layout):
        return (
            flat_values.astype(jnp.float32) + incoming[target, read_slot].astype(jnp.float32)
        ).reshape(layout)

    load_values = gap_loads.astype(jnp.float32)
    signed_gap = (orient * load_values).astype(jnp.bfloat16)
    gap_flat, gap_send = outgoing_of(signed_gap, jnp.bfloat16)
    residual = combine_rows(
        gap_flat,
        lax.all_to_all(gap_send, SUB, split_axis=0, concat_axis=0, tiled=True),
        load_values.shape,
    )
    panels = jnp.stack(
        [
            whole_panel(factors[member], coupling[member], dof_blocks[member])
            for member in range(subdomains)
        ]
    )
    multipliers = jnp.zeros_like(residual)
    for iteration in range(ITERS):
        multipliers = multipliers + STEP_SIZE * residual
        signed = (orient * multipliers).astype(jnp.bfloat16)
        panel_image = jnp.einsum("sij,sjc->sic", panels, signed, preferred_element_type=jnp.float32)
        local_term = load_values - panel_image
        flat_values, outgoing = outgoing_of(orient * local_term, jnp.float32)
        combined = combine_rows(
            flat_values,
            lax.all_to_all(
                outgoing.astype(jnp.bfloat16), SUB, split_axis=0, concat_axis=0, tiled=True
            ).astype(outgoing.dtype),
            load_values.shape,
        )
        residual = combined
    partial_value = jnp.sum(residual * residual, axis=(0, 1))
    squares_sum = by_axis(partial_value, SUB)
    residual_rms = jnp.sqrt(squares_sum / (row_count * devices) + 1e-06)
    return (multipliers, residual, residual_rms)


def solution(mesh):
    finer = Mesh(
        mesh.devices.reshape(mesh.shape["grp"], 16, 4, 2), ("grp", "sub_0", "sub_1", "sub_2")
    )
    in_specs = (
        P(GRP_SUB, None, None),
        P(GRP_SUB, None, None),
        P(GRP_SUB, None, None),
        P(GRP_SUB),
        P(GRP_SUB, None),
    )
    out_specs = (P(GRP_SUB, None, None), P(GRP_SUB, None, None), P("grp"))
    return jax.shard_map(local, mesh=finer, in_specs=in_specs, out_specs=out_specs, check_vma=False)
```

profile of v0, /device:TPU:33, one launch (start us, length us, event | category | flops | bytes accessed | tf_op | source)
XLA Modules:
  0.0 438.4 jit_solution(2306093444085306577)
XLA Ops:
  2.8 4.5 %convert_reduce_fusion = (s32[1536]{0:T(1024)S(1)}, s32[1536]{0:T(1024)S(1)}) fusion(s32[1536]{0:T(1024)S(1)} %get-tuple-element.14, s32[1536]{0:T(1024)S(1)} %get-tuple-element.13), kind=kLoop, calls=%fused_computation.10 | loop fusion | flops 21230592 | bytes 24576 | tf_op jit(solution)/shard_map/reduce_sum | solution.py:57
  11.0 8.2 %scatter_custom_fusion = bf16[2048,256]{1,0:T(8,128)(2,1)} fusion(s32[1536]{0:T(1024)S(1)} %broadcast_select_fusion, bf16[1536,256]{1,0:T(8,128)(2,1)S(1)} %bitcast.85, bf16[]{:T(256)} %constant.17.clone.1), kind=kCustom, calls=%fused_computation.74 | custom fusion | bytes 1048578
  19.2 31.6 %all-to-all-start = ((bf16[128,16,256]{2,1,0:T(8,128)(2,1)}), bf16[128,16,256]{2,1,0:T(8,128)(2,1)S(1)}, u32[]{:S(2)}, u32[]{:S(2)}) async-start(bf16[128,16,256]{2,1,0:T(8,128)(2,1)} %bitcast.1), calls=%async_computation | async-start | bytes 2097152 | tf_op jit(solution)/shard_map/all_to_all | solution.py:76
  53.5 6.0 %fusion.20 = bf16[1,512,512]{2,1,0:T(8,128)(2,1)S(1)} fusion(bf16[3,1024,1024]{2,1,0:T(8,128)(2,1)} %param.5, bf16[3,1024,512]{2,1,0:T(8,128)(2,1)} %param.6, pred[1024]{0:T(1024)(128)(4,1)S(1)} %iota_compare_fusion.2), kind=kOutput, calls=%fused_computation.45 | convolution fusion | flops 1612447744 | bytes 3672064 | tf_op jit(solution)/shard_map/dot_general | solution.py:34
  59.4 6.7 %fusion.21 = bf16[1,512,512]{2,1,0:T(8,128)(2,1)} fusion(bf16[3,1024,1024]{2,1,0:T(8,128)(2,1)} %param.5, bf16[3,1024,512]{2,1,0:T(8,128)(2,1)} %param.6, pred[1024]{0:T(1024)(128)(4,1)S(1)} %iota_compare_fusion.1), kind=kOutput, calls=%fused_computation.46 | convolution fusion | flops 1612447744 | bytes 3672064 | tf_op jit(solution)/shard_map/dot_general | solution.py:34
  66.1 6.6 %fusion.19 = bf16[1,512,512]{2,1,0:T(8,128)(2,1)} fusion(bf16[3,1024,1024]{2,1,0:T(8,128)(2,1)} %param.5, bf16[3,1024,512]{2,1,0:T(8,128)(2,1)} %param.6, pred[1024]{0:T(1024)(128)(4,1)S(1)} %iota_compare_fusion.3), kind=kOutput, calls=%fused_computation.44 | convolution fusion | flops 1612447744 | bytes 3672064 | tf_op jit(solution)/shard_map/dot_general | solution.py:34
  72.7 28.6 %all-to-all-done = bf16[128,16,256]{2,1,0:T(8,128)(2,1)S(1)} async-done(((bf16[128,16,256]{2,1,0:T(8,128)(2,1)}), bf16[128,16,256]{2,1,0:T(8,128)(2,1)S(1)}, u32[]{:S(2)}, u32[]{:S(2)}) %all-to-all-start) | async-done | bytes 1048608 | tf_op jit(solution)/shard_map/all_to_all | solution.py:76
  101.4 8.4 %gather_fusion = bf16[1536,256]{1,0:T(8,128)(2,1)S(1)} fusion(bf16[128,16,256]{2,1,0:T(8,128)(2,1)S(1)} %all-to-all-done, s32[1536]{0:T(1024)S(1)} %get-tuple-element.9), kind=kCustom, calls=%fused_computation | custom fusion | bytes 1585152 | tf_op jit(solution)/shard_map/gather | solution.py:68
  109.8 3.5 fusion.10
  113.3 7.9 %scatter_custom_fusion.1 = f32[2048,256]{1,0:T(8,128)S(1)} fusion(s32[1536]{0:T(1024)S(1)} %broadcast_select_fusion, f32[1536,256]{1,0:T(8,128)} %bitcast.82, f32[]{:T(128)} %constant.56.clone.1), kind=kCustom, calls=%fused_computation.54 | custom fusion | bytes 2097664
  121.3 62.5 %all_to_all.20 = bf16[128,16,256]{2,1,0:T(8,128)(2,1)S(1)} all-to-all(bf16[128,16,256]{2,1,0:T(8,128)(2,1)S(1)} %bitcast.76), channel_id=1, replica_groups=mesh['grp'=2,'sub_0'=16,'sub_1'=4,'sub_2'=2] {'sub_0','sub_1','sub_2'}, dimensions={0} | all-to-all | bytes 2097152 | tf_op jit(solution)/shard_map/all_to_all | solution.py:94
  184.1 18.0 %gather_fusion.1 = f32[1536,256]{1,0:T(8,128)} fusion(f32[128,16,256]{2,1,0:T(8,128)S(1)} %convert_element_type.86, s32[1536]{0:T(1024)S(1)} %get-tuple-element.9), kind=kCustom, calls=%fused_computation.1 | custom fusion | bytes 3158016 | tf_op jit(solution)/shard_map/gather | solution.py:68
  202.2 4.5 %fusion.11 = f32[3,512,256]{2,1,0:T(8,128)} fusion(bf16[3,512,256]{2,1,0:T(8,128)(2,1)S(1)} %copy-done, f32[3,512]{1,0:T(4,128)S(1)} %get-tuple-element.11, f32[3,512]{1,0:T(4,128)S(1)} %get-tuple-element.12, f32[3,512,256]{2,1,0:T(8,128)} %fusion.10, f32[3,512,256]{2,1,0:T(8,128)} %bitcast.72, bf16[3,512,256]{2,1,0:T(8,128)(2,1)} %bitcast.80, ...), kind=kOutput, calls=%fused_computation.31 | convolution fusion | flops 409337856 | bytes 7876608 | tf_op jit(solution)/shard_map/sij,sjc->sic/dot_general | solution.py:89
  206.7 7.9 %scatter_custom_fusion.2 = f32[2048,256]{1,0:T(8,128)S(1)} fusion(s32[1536]{0:T(1024)S(1)} %broadcast_select_fusion, f32[1536,256]{1,0:T(8,128)} %bitcast.84, f32[]{:T(128)} %constant.56.clone.1), kind=kCustom, calls=%fused_computation.52 | custom fusion | bytes 2097664
  214.7 62.8 %all_to_all.21 = bf16[128,16,256]{2,1,0:T(8,128)(2,1)S(1)} all-to-all(bf16[128,16,256]{2,1,0:T(8,128)(2,1)S(1)} %bitcast.77), channel_id=1, replica_groups=mesh['grp'=2,'sub_0'=16,'sub_1'=4,'sub_2'=2] {'sub_0','sub_1','sub_2'}, dimensions={0} | all-to-all | bytes 2097152 | tf_op jit(solution)/shard_map/all_to_all | solution.py:94
  277.8 18.0 %gather_fusion.2 = f32[1536,256]{1,0:T(8,128)} fusion(f32[128,16,256]{2,1,0:T(8,128)S(1)} %convert_element_type.89, s32[1536]{0:T(1024)S(1)} %get-tuple-element.9), kind=kCustom, calls=%fused_computation.2 | custom fusion | bytes 3158016 | tf_op jit(solution)/shard_map/gather | solution.py:68
  295.8 4.8 %broadcast_multiply_fusion = (f32[3,512,256]{2,1,0:T(8,128)}, f32[3,512,256]{2,1,0:T(8,128)S(1)}) fusion(f32[3,512,256]{2,1,0:T(8,128)} %fusion.11, f32[3,512,256]{2,1,0:T(8,128)} %bitcast.74, f32[3,512,256]{2,1,0:T(8,128)} %fusion.10, f32[3,512,256]{2,1,0:T(8,128)} %bitcast.73, bf16[3,512,256]{2,1,0:T(8,128)(2,1)} %bitcast.81, ...), kind=kLoop, calls=%fused_computation.70 | loop fusion | flops 4325376 | bytes 11016192 | tf_op jit(solution)/shard_map/add | solution.py:87
  302.5 7.9 %scatter_custom_fusion.3 = f32[2048,256]{1,0:T(8,128)S(1)} fusion(s32[1536]{0:T(1024)S(1)} %broadcast_select_fusion, f32[1536,256]{1,0:T(8,128)} %bitcast.83, f32[]{:T(128)} %constant.56.clone.1), kind=kCustom, calls=%fused_computation.50 | custom fusion | bytes 2097664
  310.5 62.5 %all_to_all.22 = bf16[128,16,256]{2,1,0:T(8,128)(2,1)S(1)} all-to-all(bf16[128,16,256]{2,1,0:T(8,128)(2,1)S(1)} %bitcast.78), channel_id=1, replica_groups=mesh['grp'=2,'sub_0'=16,'sub_1'=4,'sub_2'=2] {'sub_0','sub_1','sub_2'}, dimensions={0} | all-to-all | bytes 2097152 | tf_op jit(solution)/shard_map/all_to_all | solution.py:94
  373.3 18.0 %gather_fusion.3 = f32[1536,256]{1,0:T(8,128)} fusion(f32[128,16,256]{2,1,0:T(8,128)S(1)} %convert_element_type.92, s32[1536]{0:T(1024)S(1)} %get-tuple-element.9), kind=kCustom, calls=%fused_computation.3 | custom fusion | bytes 3158016 | tf_op jit(solution)/shard_map/gather | solution.py:68
  391.3 3.2 multiply_reduce_fusion
  394.5 24.6 %psum.21 = f32[256]{0:T(256)S(1)} all-reduce(f32[256]{0:T(256)S(1)} %get-tuple-element.5), channel_id=1, replica_groups=mesh['grp'=2,'sub_0'=16,'sub_1'=4,'sub_2'=2] {'sub_0'}, use_global_device_ids=true, to_apply=%region_7.8 | all-reduce | flops 256 | bytes 2048 | tf_op jit(solution)/shard_map/psum | solution.py:20
  419.1 7.4 %psum.22 = f32[256]{0:T(256)S(1)} all-reduce(f32[256]{0:T(256)S(1)} %psum.21), channel_id=1, replica_groups=mesh['grp'=2,'sub_0'=16,'sub_1'=4,'sub_2'=2] {'sub_1'}, use_global_device_ids=true, to_apply=%region_8.9 | all-reduce | flops 256 | bytes 2048 | tf_op jit(solution)/shard_map/psum | solution.py:20
  426.5 11.0 %psum.23 = f32[256]{0:T(256)S(1)} all-reduce(f32[256]{0:T(256)S(1)} %psum.22), channel_id=1, replica_groups=mesh['grp'=2,'sub_0'=16,'sub_1'=4,'sub_2'=2] {'sub_2'}, use_global_device_ids=true, to_apply=%region_9.10 | all-reduce | flops 256 | bytes 2048 | tf_op jit(solution)/shard_map/psum | solution.py:20
  (34 shorter events, 10.2 us)
Async XLA Ops:
  11.0 39.8 %copy-start.2 = (s32[3]{0:T(128)S(1)}, s32[3]{0:T(128)}, u32[]{:S(2)}) copy-start(s32[3]{0:T(128)} %param.8) | copy-start | bytes 40
  19.2 82.2 %all-to-all-start = ((bf16[128,16,256]{2,1,0:T(8,128)(2,1)}), bf16[128,16,256]{2,1,0:T(8,128)(2,1)S(1)}, u32[]{:S(2)}, u32[]{:S(2)}) async-start(bf16[128,16,256]{2,1,0:T(8,128)(2,1)} %bitcast.1), calls=%async_computation | async-start | bytes 2097152 | tf_op jit(solution)/shard_map/all_to_all | solution.py:76
  101.3 8.4 %copy-start = (bf16[3,512,256]{2,1,0:T(8,128)(2,1)S(1)}, bf16[3,512,256]{2,1,0:T(8,128)(2,1)}, u32[]{:S(2)}) copy-start(bf16[3,512,256]{2,1,0:T(8,128)(2,1)} %param.7) | copy-start | bytes 2359300
  109.8 3.6 copy-start.1
  295.8 4.8 %copy-start.3 = (bf16[1,512,512]{2,1,0:T(8,128)(2,1)S(1)}, bf16[1,512,512]{2,1,0:T(8,128)(2,1)}, u32[]{:S(2)}) copy-start(bf16[1,512,512]{2,1,0:T(8,128)(2,1)} %fusion.21) | copy-start | bytes 1572868
  295.8 4.8 %copy-start.4 = (bf16[1,512,512]{2,1,0:T(8,128)(2,1)S(1)}, bf16[1,512,512]{2,1,0:T(8,128)(2,1)}, u32[]{:S(2)}) copy-start(bf16[1,512,512]{2,1,0:T(8,128)(2,1)} %fusion.19) | copy-start | bytes 1572868
where the time goes:
time: 445 us; the launch traced here: 438 us
  blocking collectives  231 us (52%)
  local copies, waits for them, and re-layouts  95.6 us (21%)
  starting transfers between devices  31.6 us (7%)
  matrix products  29.2 us (7%)
  waiting for transfers between devices  28.6 us (6%)
  other arithmetic  19.4 us (4%)
    all_to_all x3, blocking collectives, local(): lax.all_to_all(outgoing.astype(jnp.bfloat16), SUB, split_axis=0, concat_a...  188 us
    gather x4, local copies, waits for them, and re-layouts, combine_rows(): incoming[target, read_slot].astype(jnp.float32)  62.4 us
    psum x3, blocking collectives, by_axis(): return functools.reduce(lax.psum, axes, value)  42.9 us
    unnamed x16, local copies, waits for them, and re-layouts  31.8 us
    all_to_all x1, starting transfers between devices, local(): lax.all_to_all(gap_send, SUB, split_axis=0, concat_axis=0, tiled=True)  31.6 us
    all_to_all x1, waiting for transfers between devices, local(): lax.all_to_all(gap_send, SUB, split_axis=0, concat_axis=0, tiled=True)  28.6 us
    dot_general x3, matrix products, whole_panel(): lax.dot_general(reduced, reduced, (((0,), (0,)), ((), ())), preferred_ele...  19.3 us
    dot_general x3, matrix products, local(): jnp.einsum('sij,sjc->sic', panels, signed, preferred_element_type=jnp.flo...  9.93 us
  transfers between devices with their start and end apart: 1, of which 1 were waited for; matrix products, arithmetic and copies ran while one was open for 5% of the time, Pallas kernels for 0%

commit v1 on v0

v1 whole, which is shorter than its diff:
```python
import jax
import jax.numpy as jnp
from jax import lax
from jax.experimental import pallas as pl
from jax.experimental.pallas import tpu as pltpu
from jax.sharding import Mesh
from jax.sharding import PartitionSpec as P

DBLK = 128
FROWS = 16
ITERS = 3
LANES = 128
TILE = 512
SUB = ("sub_0", "sub_1", "sub_2")
GRP_SUB = ("grp", "sub_0", "sub_1", "sub_2")

STEP_SIZE = 0.25
F32 = jnp.float32
BF16 = jnp.bfloat16


def whole_panel(factor, couple, blocks):
    present = jnp.arange(couple.shape[0]) < blocks * DBLK
    masked = jnp.where(present[:, None], couple, jnp.zeros_like(couple))
    product = lax.dot_general(
        factor, masked, (((0,), (0,)), ((), ())), preferred_element_type=F32
    )
    reduced = jnp.where(present[:, None], product, jnp.zeros_like(product)).astype(BF16)
    schur_panel = lax.dot_general(
        reduced, reduced, (((0,), (0,)), ((), ())), preferred_element_type=F32
    )
    return schur_panel.astype(BF16)


def total_over_group(part):
    for axes in (("sub_0",), ("sub_1", "sub_2")):
        copies = jnp.broadcast_to(part[None], (lax.axis_size(axes),) + part.shape)
        part = jnp.sum(lax.all_to_all(copies, axes, 0, 0, tiled=True), axis=0)
    return part


def place_rows(slot_ref, values_ref, send_ref):
    rows = values_ref.shape[0]

    def body(q, carry):
        base = pl.multiple_of(q * TILE, TILE)
        ids = lax.broadcasted_iota(jnp.int32, (TILE, rows), 0) + base
        chosen = jnp.where(ids == slot_ref[...], 1.0, 0.0).astype(BF16)
        placed = jnp.dot(chosen, values_ref[...], preferred_element_type=F32)
        send_ref[pl.ds(base, TILE), :] = placed.astype(BF16)
        return carry

    lax.fori_loop(0, send_ref.shape[0] // TILE, body, 0)


def landed_rows(slot_col_ref, incoming_ref, base):
    slots = incoming_ref.shape[0]
    column = slot_col_ref[pl.ds(base, TILE), :]
    pieces = []
    lane = lax.broadcasted_iota(jnp.int32, (TILE, LANES), 1)
    for t in range(slots // LANES):
        pieces.append(jnp.where(lane + t * LANES == column, 1.0, 0.0).astype(BF16))
    chosen = jnp.concatenate(pieces, axis=1)
    return jnp.dot(chosen, incoming_ref[...], preferred_element_type=F32)


def open_kernel(position_ref, partner_ref, gap_ref, send_ref, slot_ref, order_ref, sign_ref, comp):
    subdomains, interface = partner_ref.shape
    rows = subdomains * interface
    tiles = rows // LANES
    per = interface // LANES
    span = pl.next_power_of_2(rows)
    partner = jnp.concatenate(
        [
            partner_ref[s : s + 1, t * LANES : (t + 1) * LANES]
            for s in range(subdomains)
            for t in range(per)
        ],
        axis=0,
    )
    target = jnp.floor((partner.astype(F32) + 0.5) * (1.0 / rows))
    remote = partner.astype(F32) - target * rows
    ordinal = (
        lax.broadcasted_iota(jnp.int32, (tiles, LANES), 0) * LANES
        + lax.broadcasted_iota(jnp.int32, (tiles, LANES), 1)
    ).astype(F32)
    lower = position_ref[0].astype(F32) < target
    first = target * span
    full = first + jnp.where(lower, ordinal, remote)
    for t in range(tiles):
        comp[t * LANES : (t + 1) * LANES, :] = jnp.broadcast_to(
            full[t : t + 1, :], (LANES, LANES)
        ).T
    ranks = []
    for t in range(tiles):
        lo, hi = first[t : t + 1, :], full[t : t + 1, :]

        def count(j, acc, lo=lo, hi=hi):
            other = comp[pl.ds(pl.multiple_of(j * LANES, LANES), LANES), :]
            ahead = jnp.where((other >= lo) & (other < hi), 1.0, 0.0)
            return acc + jnp.sum(ahead.reshape(LANES // 8, 8, LANES), axis=0)

        acc = lax.fori_loop(0, tiles, count, jnp.zeros((8, LANES), F32))
        ranks.append(jnp.sum(acc, axis=0, keepdims=True))
    slot = (target * FROWS + jnp.concatenate(ranks, axis=0)).astype(jnp.int32)
    order_ref[...] = slot
    sign_ref[...] = jnp.where(lower, 1.0, -1.0)
    for t in range(tiles):
        slot_ref[:, t * LANES : (t + 1) * LANES] = slot[t : t + 1, :]
    place_rows(slot_ref, gap_ref, send_ref)


def step_kernel(incoming_ref, own_ref, mult_ref, gap_ref, panel_ref, slot_ref, slot_col_ref, sign_ref,
                send_ref, own_out, mult_out, own_bf):
    def body(s, carry):
        base = pl.multiple_of(s * TILE, TILE)
        here = pl.ds(base, TILE)
        sign = jnp.concatenate([sign_ref[here, :]] * (own_ref.shape[1] // LANES), axis=1)
        residual = own_ref[here, :] - landed_rows(slot_col_ref, incoming_ref, base)
        mult = mult_ref[here, :] + (STEP_SIZE * sign) * residual
        mult_out[here, :] = mult
        signed = (sign * mult).astype(BF16)
        image = jnp.dot(panel_ref[s], signed, preferred_element_type=F32)
        own = gap_ref[here, :].astype(F32) - image
        own_out[here, :] = own
        own_bf[here, :] = own.astype(BF16)
        return carry

    lax.fori_loop(0, own_ref.shape[0] // TILE, body, 0)
    place_rows(slot_ref, own_bf, send_ref)


def close_kernel(incoming_ref, own_ref, slot_col_ref, sign_ref, residual_ref, squares_ref):
    columns = own_ref.shape[1]

    def body(s, acc):
        base = pl.multiple_of(s * TILE, TILE)
        here = pl.ds(base, TILE)
        sign = jnp.concatenate([sign_ref[here, :]] * (columns // LANES), axis=1)
        residual = own_ref[here, :] - landed_rows(slot_col_ref, incoming_ref, base)
        residual_ref[here, :] = sign * residual
        return acc + jnp.sum((residual * residual).reshape(TILE // 8, 8, columns), axis=0)

    acc = lax.fori_loop(0, own_ref.shape[0] // TILE, body, jnp.zeros((8, columns), F32))
    squares_ref[...] = jnp.sum(acc, axis=0, keepdims=True)


def vmem_call(kernel, outs, n_in, scratch=(), smem_first=False, aliases=None, flops=0):
    spec = pl.BlockSpec(memory_space=pltpu.VMEM)
    in_specs = [spec] * n_in
    if smem_first:
        in_specs[0] = pl.BlockSpec(memory_space=pltpu.SMEM)
    return pl.pallas_call(
        kernel,
        out_shape=[jax.ShapeDtypeStruct(s, d) for s, d in outs],
        in_specs=in_specs,
        out_specs=[spec] * len(outs),
        scratch_shapes=list(scratch),
        input_output_aliases=aliases or {},
        cost_estimate=pl.CostEstimate(flops=flops, bytes_accessed=8 << 20, transcendentals=0),
        compiler_params=pltpu.CompilerParams(vmem_limit_bytes=40 << 20),
    )


def local(factors, coupling, gap_loads, dof_blocks, partner_rows):
    subdomains, interface, columns = gap_loads.shape
    devices = lax.axis_size(SUB)
    position = lax.axis_index(SUB)
    rows = subdomains * interface
    slots = devices * FROWS
    tiles = rows // LANES
    gap = gap_loads.reshape(rows, columns)

    def exchange(outgoing):
        blocks = outgoing.reshape(devices, FROWS, columns)
        return lax.all_to_all(blocks, SUB, split_axis=0, concat_axis=0, tiled=True).reshape(
            slots, columns
        )

    outgoing, slot, order, sign = vmem_call(
        open_kernel,
        [((slots, columns), BF16), ((1, rows), jnp.int32), ((tiles, LANES), jnp.int32), ((tiles, LANES), F32)],
        3,
        scratch=[pltpu.VMEM((rows, LANES), F32)],
        smem_first=True,
        flops=2 * slots * rows * columns,
    )(position.astype(jnp.int32).reshape(1), partner_rows, gap)
    incoming = exchange(outgoing)
    panels = jnp.stack(
        [whole_panel(factors[s], coupling[s], dof_blocks[s]) for s in range(subdomains)]
    )
    slot_col = jnp.broadcast_to(order.reshape(rows, 1), (rows, LANES))
    sign_col = jnp.broadcast_to(sign.reshape(rows, 1), (rows, LANES))
    step = vmem_call(
        step_kernel,
        [((slots, columns), BF16), ((rows, columns), F32), ((rows, columns), F32)],
        8,
        scratch=[pltpu.VMEM((rows, columns), BF16)],
        aliases={1: 1, 2: 2},
        flops=4 * slots * rows * columns,
    )

    def iteration(_, carry):
        incoming, own, multipliers = carry
        outgoing, own, multipliers = step(
            incoming, own, multipliers, gap, panels, slot, slot_col, sign_col
        )
        return exchange(outgoing), own, multipliers

    carry = (incoming, gap.astype(F32), jnp.zeros((rows, columns), F32))
    for k in range(ITERS):
        carry = iteration(k, carry)
    incoming, own, multipliers = carry
    residual, squares = vmem_call(
        close_kernel, [((rows, columns), F32), ((1, columns), F32)], 4, flops=2 * slots * rows * columns
    )(incoming, own, slot_col, sign_col)
    squares = total_over_group(squares).reshape(columns)
    shape = (subdomains, interface, columns)
    return (
        multipliers.reshape(shape),
        residual.reshape(shape),
        jnp.sqrt(squares / (rows * devices) + 1e-06),
    )


def solution(mesh):
    finer = Mesh(
        mesh.devices.reshape(mesh.shape["grp"], 16, 4, 2), ("grp", "sub_0", "sub_1", "sub_2")
    )
    in_specs = (
        P(GRP_SUB, None, None),
        P(GRP_SUB, None, None),
        P(GRP_SUB, None, None),
        P(GRP_SUB),
        P(GRP_SUB, None),
    )
    out_specs = (P(GRP_SUB, None, None), P(GRP_SUB, None, None), P("grp"))
    return jax.shard_map(local, mesh=finer, in_specs=in_specs, out_specs=out_specs, check_vma=False)
```

time: 445 us -> 337 us (0.76); the launches traced: 438 us -> 336 us
  local copies, waits for them, and re-layouts: 95.6 us -> 5.21 us
  Pallas kernels: 0 us -> 33.8 us
  other arithmetic: 19.4 us -> 1 us
  blocking collectives: 231 us -> 215 us
  matrix products: 29.2 us -> 17.6 us
    gather x4 -> x0, local copies, waits for them, and re-layouts: 62.4 us -> none  [combine_rows(): incoming[target, read_slot].astype(jnp.float32)]
    psum x3 -> x0, blocking collectives: 42.9 us -> none  [by_axis(): return functools.reduce(lax.psum, axes, value)]
    pallas_call x0 -> x5, Pallas kernels: none -> 33.8 us  [the longest x3 23.9 us: iteration(): step(incoming, own, multipliers, gap, panels, slot, slot_col, sign_col)]
    unnamed x16 -> x10, local copies, waits for them, and re-layouts: 31.8 us -> 2.78 us
    all_to_all x3 -> x5, blocking collectives: 188 us -> 215 us  [the longest x3 188 us: exchange(): lax.all_to_all(blocks, SUB, split_axis=0, concat_axis=0, tiled=True)]
    dot_general x3 -> x0, matrix products: 9.93 us -> none  [local(): jnp.einsum('sij,sjc->sic', panels, signed, preferred_element_type=jnp.flo...]
    reduce_sum x2, other arithmetic: 7.72 us -> 0.06 us  [total_over_group(): part = jnp.sum(lax.all_to_all(copies, axes, 0, 0, tiled=True), axis=0)]
    add x1 -> x0, other arithmetic: 4.82 us -> none  [local(): multipliers = multipliers + STEP_SIZE * residual]
  transfers between devices with their start and end apart: 1 -> 1, of which waited for: 1 -> 1; matrix products, arithmetic and copies ran while one was open for 5% -> 6% of each run, Pallas kernels for 0% -> 0%
where the time goes in v1:
time: 337 us; the launch traced here: 336 us
  blocking collectives  215 us (64%)
  Pallas kernels  33.8 us (10%)
  starting transfers between devices  31.2 us (9%)
  waiting for transfers between devices  29.4 us (9%)
  matrix products  17.6 us (5%)
  local copies, waits for them, and re-layouts  5.21 us (2%)
    all_to_all x3, blocking collectives, exchange(): lax.all_to_all(blocks, SUB, split_axis=0, concat_axis=0, tiled=True)  188 us
    all_to_all x1, starting transfers between devices, exchange(): lax.all_to_all(blocks, SUB, split_axis=0, concat_axis=0, tiled=True)  31.2 us
    all_to_all x1, waiting for transfers between devices, exchange(): lax.all_to_all(blocks, SUB, split_axis=0, concat_axis=0, tiled=True)  29.4 us
    all_to_all x2, blocking collectives, total_over_group(): part = jnp.sum(lax.all_to_all(copies, axes, 0, 0, tiled=True), axis=0)  27.4 us
    pallas_call x3, Pallas kernels, iteration(): step(incoming, own, multipliers, gap, panels, slot, slot_col, sign_col)  23.9 us
    dot_general x3, matrix products, whole_panel(): lax.dot_general(reduced, reduced, (((0,), (0,)), ((), ())), preferred_ele...  17.6 us
  transfers between devices with their start and end apart: 1, of which 1 were waited for; matrix products, arithmetic and copies ran while one was open for 6% of the time, Pallas kernels for 0%

profile of v1, /device:TPU:33, one launch (start us, length us, event | category | flops | bytes accessed | tf_op | source)
XLA Modules:
  0.0 335.9 jit_solution(16121915744704881707)
XLA Ops:
  0.6 1.1 copy-done
  1.8 0.7 copy-done.3
  2.5 6.6 %shard_map.76 = (bf16[2048,256]{1,0:T(8,128)(2,1)}, s32[1,1536]{1,0:T(1,128)S(1)}, s32[12,128]{1,0:T(8,128)S(1)}, f32[12,128]{1,0:T(8,128)S(1)}) custom-call(s32[1]{0:T(128)} %bitcast.position_ref, s32[3,512]{1,0:T(4,128)S(1)} %copy-done.3, bf16[1536,256]{1,0:T(8,128)(2,1)S(1)} %bitcast.67), custom_call_target="tpu_custom_call" | custom-call | flops 1610612736 | bytes 8388608 | tf_op jit(solution)/shard_map/pallas_call | solution.py:180
  9.1 31.2 %all-to-all-start = ((bf16[128,16,256]{2,1,0:T(8,128)(2,1)}), bf16[128,16,256]{2,1,0:T(8,128)(2,1)}, u32[]{:S(2)}, u32[]{:S(2)}) async-start(bf16[128,16,256]{2,1,0:T(8,128)(2,1)} %bitcast.2), calls=%async_computation | async-start | bytes 2097152 | tf_op jit(solution)/shard_map/all_to_all | solution.py:176
  40.3 0.6 fusion.68
  42.9 5.9 %fusion.16 = bf16[1,512,512]{2,1,0:T(8,128)(2,1)S(1)} fusion(bf16[3,1024,1024]{2,1,0:T(8,128)(2,1)} %param.5, bf16[3,1024,512]{2,1,0:T(8,128)(2,1)} %param.6, pred[1024]{0:T(1024)(128)(4,1)S(1)} %iota_compare_fusion.1), kind=kOutput, calls=%fused_computation.17 | convolution fusion | flops 1612447744 | bytes 3672064 | tf_op jit(solution)/shard_map/dot_general | solution.py:29
  48.8 5.9 %fusion.17 = bf16[1,512,512]{2,1,0:T(8,128)(2,1)S(1)} fusion(bf16[3,1024,1024]{2,1,0:T(8,128)(2,1)} %param.5, bf16[3,1024,512]{2,1,0:T(8,128)(2,1)} %param.6, pred[1024]{0:T(1024)(128)(4,1)S(1)} %iota_compare_fusion), kind=kOutput, calls=%fused_computation.18 | convolution fusion | flops 1612447744 | bytes 3672064 | tf_op jit(solution)/shard_map/dot_general | solution.py:29
  54.6 5.9 %fusion.15 = bf16[1,512,512]{2,1,0:T(8,128)(2,1)S(1)} fusion(bf16[3,1024,1024]{2,1,0:T(8,128)(2,1)} %param.5, bf16[3,1024,512]{2,1,0:T(8,128)(2,1)} %param.6, pred[1024]{0:T(1024)(128)(4,1)S(1)} %iota_compare_fusion.2), kind=kOutput, calls=%fused_computation.16 | convolution fusion | flops 1612447744 | bytes 3672064 | tf_op jit(solution)/shard_map/dot_general | solution.py:29
  60.6 0.2 pad_maximum_fusion.panel_ref
  60.8 0.9 copy-done.1
  61.9 29.4 %all-to-all-done = bf16[128,16,256]{2,1,0:T(8,128)(2,1)} async-done(((bf16[128,16,256]{2,1,0:T(8,128)(2,1)}), bf16[128,16,256]{2,1,0:T(8,128)(2,1)}, u32[]{:S(2)}, u32[]{:S(2)}) %all-to-all-start) | async-done | bytes 1048608 | tf_op jit(solution)/shard_map/all_to_all | solution.py:176
  91.3 0.3 broadcast_in_dim.81.slot_col_ref
  91.6 0.3 broadcast_in_dim.83.sign_ref
  91.8 1.3 broadcast_in_dim.73.mult_ref
  93.1 8.2 %shard_map.77 = (bf16[2048,256]{1,0:T(8,128)(2,1)S(1)}, f32[1536,256]{1,0:T(8,128)S(1)}, f32[1536,256]{1,0:T(8,128)}) custom-call(bf16[2048,256]{1,0:T(8,128)(2,1)} %bitcast.3.incoming_ref, f32[1536,256]{1,0:T(8,128)S(1)} %bitcast_convert_fusion.own_ref, f32[1536,256]{1,0:T(8,128)} %broadcast_in_dim.73.mult_ref, ...), custom_call_target="tpu_custom_call", output_to_operand_aliasing={{1}: (1, {}), {2}: (2, {})} | custom-call | flops 3221225472 | bytes 8388608 | tf_op jit(solution)/shard_map/pallas_call | solution.py:205
  101.3 62.5 %all_to_all.30 = bf16[128,16,256]{2,1,0:T(8,128)(2,1)S(1)} all-to-all(bf16[128,16,256]{2,1,0:T(8,128)(2,1)S(1)} %bitcast.64), channel_id=1, replica_groups=mesh['grp'=2,'sub_0'=16,'sub_1'=4,'sub_2'=2] {'sub_0','sub_1','sub_2'}, dimensions={0} | all-to-all | bytes 2097152 | tf_op jit(solution)/shard_map/all_to_all | solution.py:176
  163.8 7.9 %shard_map.78 = (bf16[2048,256]{1,0:T(8,128)(2,1)S(1)}, f32[1536,256]{1,0:T(8,128)S(1)}, f32[1536,256]{1,0:T(8,128)}) custom-call(bf16[2048,256]{1,0:T(8,128)(2,1)S(1)} %bitcast.63, f32[1536,256]{1,0:T(8,128)S(1)} %get-tuple-element.23.own_ref, f32[1536,256]{1,0:T(8,128)} %get-tuple-element.24.mult_ref, ...), custom_call_target="tpu_custom_call", output_to_operand_aliasing={{1}: (1, {}), {2}: (2, {})} | custom-call | flops 3221225472 | bytes 8388608 | tf_op jit(solution)/shard_map/pallas_call | solution.py:205
  171.7 62.5 %all_to_all.31 = bf16[128,16,256]{2,1,0:T(8,128)(2,1)S(1)} all-to-all(bf16[128,16,256]{2,1,0:T(8,128)(2,1)S(1)} %bitcast.65), channel_id=1, replica_groups=mesh['grp'=2,'sub_0'=16,'sub_1'=4,'sub_2'=2] {'sub_0','sub_1','sub_2'}, dimensions={0} | all-to-all | bytes 2097152 | tf_op jit(solution)/shard_map/all_to_all | solution.py:176
  234.2 7.9 %shard_map.79 = (bf16[2048,256]{1,0:T(8,128)(2,1)S(1)}, f32[1536,256]{1,0:T(8,128)S(1)}, f32[1536,256]{1,0:T(8,128)}) custom-call(bf16[2048,256]{1,0:T(8,128)(2,1)S(1)} %bitcast.61, f32[1536,256]{1,0:T(8,128)S(1)} %get-tuple-element.26.own_ref, f32[1536,256]{1,0:T(8,128)} %get-tuple-element.27.mult_ref, ...), custom_call_target="tpu_custom_call", output_to_operand_aliasing={{1}: (1, {}), {2}: (2, {})} | custom-call | flops 3221225472 | bytes 8388608 | tf_op jit(solution)/shard_map/pallas_call | solution.py:205
  242.1 62.5 %all_to_all.32 = bf16[128,16,256]{2,1,0:T(8,128)(2,1)S(1)} all-to-all(bf16[128,16,256]{2,1,0:T(8,128)(2,1)S(1)} %bitcast.62), channel_id=1, replica_groups=mesh['grp'=2,'sub_0'=16,'sub_1'=4,'sub_2'=2] {'sub_0','sub_1','sub_2'}, dimensions={0} | all-to-all | bytes 2097152 | tf_op jit(solution)/shard_map/all_to_all | solution.py:176
  304.6 3.3 shard_map.80
  307.9 18.5 %all_to_all.33 = f32[16,1,256]{2,1,0:T(1,128)S(1)} all-to-all(f32[16,1,256]{2,1,0:T(1,128)S(1)} %broadcast_in_dim.85), channel_id=1, replica_groups=mesh['grp'=2,'sub_0'=16,'sub_1'=4,'sub_2'=2] {'sub_0'}, dimensions={0} | all-to-all | bytes 32768 | tf_op jit(solution)/shard_map/all_to_all | solution.py:38
  326.4 8.9 %all_to_all.34 = f32[8,1,256]{2,1,0:T(1,128)S(1)} all-to-all(f32[8,1,256]{2,1,0:T(1,128)S(1)} %broadcast_in_dim.86), channel_id=1, replica_groups=mesh['grp'=2,'sub_0'=16,'sub_1'=4,'sub_2'=2] {'sub_1','sub_2'}, dimensions={0} | all-to-all | bytes 16384 | tf_op jit(solution)/shard_map/all_to_all | solution.py:38
  335.4 0.6 add_sqrt_fusion
  (15 shorter events, 0.3 us)
Async XLA Ops:
  0.6 1.1 copy-start
  1.8 0.7 copy-start.3
  9.1 31.2 %copy-start.4 = (s32[3]{0:T(128)S(1)}, s32[3]{0:T(128)}, u32[]{:S(2)}) copy-start(s32[3]{0:T(128)} %param.8) | copy-start | bytes 40
  9.1 82.2 %all-to-all-start = ((bf16[128,16,256]{2,1,0:T(8,128)(2,1)}), bf16[128,16,256]{2,1,0:T(8,128)(2,1)}, u32[]{:S(2)}, u32[]{:S(2)}) async-start(bf16[128,16,256]{2,1,0:T(8,128)(2,1)} %bitcast.2), calls=%async_computation | async-start | bytes 2097152 | tf_op jit(solution)/shard_map/all_to_all | solution.py:176
  60.6 1.1 copy-start.1
  91.3 1.8 copy-start.2

commit v2 on v1

v2 whole, which is shorter than its diff:
```python
import functools

import jax
import jax.numpy as jnp
from jax import lax
from jax.experimental import pallas as pl
from jax.experimental.pallas import tpu as pltpu
from jax.sharding import Mesh
from jax.sharding import PartitionSpec as P

DBLK = 128
FROWS = 16
ITERS = 3
LANES = 128
SUBLANES = 8
TILE = 512
SUB = ("sub_0", "sub_1", "sub_2")
GRP_SUB = ("grp", "sub_0", "sub_1", "sub_2")

STEP_SIZE = 0.25
F32 = jnp.float32
BF16 = jnp.bfloat16


def whole_panel(factor, couple, blocks):
    present = jnp.arange(couple.shape[0]) < blocks * DBLK
    masked = jnp.where(present[:, None], couple, jnp.zeros_like(couple))
    product = lax.dot_general(
        factor, masked, (((0,), (0,)), ((), ())), preferred_element_type=F32
    )
    reduced = jnp.where(present[:, None], product, jnp.zeros_like(product)).astype(BF16)
    schur_panel = lax.dot_general(
        reduced, reduced, (((0,), (0,)), ((), ())), preferred_element_type=F32
    )
    return schur_panel.astype(BF16)


def chosen_rows(slot_ref, base, count):
    ids = lax.broadcasted_iota(jnp.int32, (count, slot_ref.shape[1]), 0) + base
    return jnp.where(ids == slot_ref[...], 1.0, 0.0).astype(BF16)


def open_kernel(position_ref, partner_hbm, gap_hbm, send_ref, slot_ref, order_ref, sign_ref, partner_ref, gap_ref, comp, sems):
    load_partner = pltpu.make_async_copy(partner_hbm, partner_ref, sems.at[0])
    load_gap = pltpu.make_async_copy(gap_hbm, gap_ref, sems.at[1])
    load_partner.start()
    load_gap.start()
    load_partner.wait()
    subdomains, interface = partner_ref.shape
    rows = subdomains * interface
    tiles = rows // LANES
    span = pl.next_power_of_2(rows)
    partner = jnp.concatenate(
        [
            partner_ref[s : s + 1, t : t + LANES]
            for s in range(subdomains)
            for t in range(0, interface, LANES)
        ],
        axis=0,
    ).astype(F32)
    target = jnp.floor((partner + 0.5) * (1.0 / rows))
    remote = partner - target * rows
    ordinal = (
        lax.broadcasted_iota(jnp.int32, (tiles, LANES), 0) * LANES
        + lax.broadcasted_iota(jnp.int32, (tiles, LANES), 1)
    ).astype(F32)
    first = target * span
    lower = position_ref[0].astype(F32) < target
    sign_ref[...] = jnp.where(lower, 1.0, -1.0)
    full = first + jnp.where(lower, ordinal, remote)
    for t in range(tiles):
        comp[t * LANES : (t + 1) * LANES, :] = jnp.broadcast_to(
            full[t : t + 1, :], (LANES, LANES)
        ).T
    low = [jnp.broadcast_to(first[t : t + 1, :], (SUBLANES, LANES)) for t in range(tiles)]
    high = [jnp.broadcast_to(full[t : t + 1, :], (SUBLANES, LANES)) for t in range(tiles)]

    def count(j, acc):
        acc = list(acc)
        for k in range(4):
            other = comp[pl.ds(pl.multiple_of(j * 4 * SUBLANES, 4 * SUBLANES) + k * SUBLANES, SUBLANES), :]
            for t in range(tiles):
                acc[t] = acc[t] + jnp.where((other >= low[t]) & (other < high[t]), 1.0, 0.0)
        return tuple(acc)

    zero = jnp.zeros((SUBLANES, LANES), F32)
    acc = lax.fori_loop(0, rows // (4 * SUBLANES), count, (zero,) * tiles)
    for t in range(tiles):
        rank = jnp.sum(acc[t], axis=0, keepdims=True)
        slot = (target[t : t + 1, :] * FROWS + rank).astype(jnp.int32)
        slot_ref[:, t * LANES : (t + 1) * LANES] = slot
        order_ref[t : t + 1, :] = slot
    load_gap.wait()

    def place(q, carry):
        base = pl.multiple_of(q * TILE, TILE)
        placed = jnp.dot(chosen_rows(slot_ref, base, TILE), gap_ref[...], preferred_element_type=F32)
        send_ref[pl.ds(base, TILE), :] = placed.astype(BF16)
        return carry

    lax.fori_loop(0, send_ref.shape[0] // TILE, place, 0)


def build_kernel(slot_ref, panel_ref, matrix_ref, place_ref, half):
    slots, _ = place_ref.shape
    subdomains, interface = panel_ref.shape[:2]

    def choose(q, carry):
        base = pl.multiple_of(q * 256, 256)
        place_ref[pl.ds(base, 256), :] = chosen_rows(slot_ref, base, 256)
        return carry

    lax.fori_loop(0, slots // 256, choose, 0)

    def body(q, carry):
        here = pl.ds(pl.multiple_of(q * TILE, TILE), TILE)
        for s in range(subdomains):
            cols = slice(s * interface, (s + 1) * interface)
            half[:, cols] = jnp.dot(
                place_ref[here, cols], panel_ref[s], preferred_element_type=F32
            ).astype(BF16)
        for n in range(0, slots, 1024):
            matrix_ref[here, n : n + 1024] = lax.dot_general(
                half[...], place_ref[n : n + 1024, :], (((1,), (1,)), ((), ())), preferred_element_type=F32
            ).astype(BF16)
        return carry

    lax.fori_loop(0, slots // TILE, body, 0)


def step_kernel(*refs, first, last):
    if first:
        incoming_ref, gap_ref, matrix_ref, send_ref, next_ref, signed_ref = refs
    elif last:
        base_ref, incoming_ref, gap_ref, matrix_ref, send_ref, signed_ref = refs
    else:
        base_ref, incoming_ref, gap_ref, matrix_ref, send_ref, next_ref, signed_ref = refs

    def multipliers(here):
        base = STEP_SIZE * gap_ref[here, :].astype(F32) if first else base_ref[here, :]
        return base - STEP_SIZE * incoming_ref[here, :].astype(F32)

    tiles = [slice(q, q + TILE) for q in range(0, send_ref.shape[0], TILE)]
    for here in tiles:
        signed_ref[here, :] = multipliers(here).astype(BF16)
    for here in tiles:
        image = jnp.dot(matrix_ref[here, :], signed_ref[...], preferred_element_type=F32)
        own = gap_ref[here, :].astype(F32) - image
        send_ref[here, :] = own.astype(BF16)
        if not last:
            next_ref[here, :] = multipliers(here) + STEP_SIZE * own


def chosen_slots(column_ref, base, slots):
    column = column_ref[pl.ds(base, TILE), :]
    lane = lax.broadcasted_iota(jnp.int32, (TILE, LANES), 1)
    pieces = [
        jnp.where(lane + t == column, 1.0, 0.0).astype(BF16) for t in range(0, slots, LANES)
    ]
    return jnp.concatenate(pieces, axis=1)


def across(sign_ref, here, columns):
    return jnp.concatenate([sign_ref[here, :]] * (columns // LANES), axis=1)


def last_kernel(base_ref, incoming_ref, gap_ref, column_ref, sign_ref, panel_ref,
                own_ref, mult_ref, signed, low):
    slots, columns = signed.shape

    def split(q, carry):
        here = pl.ds(pl.multiple_of(q * TILE, TILE), TILE)
        value = base_ref[here, :] - STEP_SIZE * incoming_ref[here, :].astype(F32)
        high = value.astype(BF16)
        signed[here, :] = high
        low[here, :] = (value - high.astype(F32)).astype(BF16)
        return carry

    lax.fori_loop(0, slots // TILE, split, 0)

    def rows(s, carry):
        base = pl.multiple_of(s * TILE, TILE)
        here = pl.ds(base, TILE)
        chosen = chosen_slots(column_ref, base, slots)
        high = jnp.dot(chosen, signed[...], preferred_element_type=F32)
        rest = jnp.dot(chosen, low[...], preferred_element_type=F32)
        mult_ref[here, :] = across(sign_ref, here, columns) * (high + rest)
        image = jnp.dot(panel_ref[s], high.astype(BF16), preferred_element_type=F32)
        own_ref[here, :] = gap_ref[here, :].astype(F32) - image
        return carry

    lax.fori_loop(0, panel_ref.shape[0], rows, 0)


def close_kernel(own_ref, incoming_ref, column_ref, sign_ref, residual_ref, squares_ref):
    slots, columns = incoming_ref.shape

    def body(s, acc):
        base = pl.multiple_of(s * TILE, TILE)
        here = pl.ds(base, TILE)
        landed = jnp.dot(
            chosen_slots(column_ref, base, slots), incoming_ref[...], preferred_element_type=F32
        )
        residual = own_ref[here, :] - landed
        residual_ref[here, :] = across(sign_ref, here, columns) * residual
        return acc + jnp.sum((residual * residual).reshape(TILE // SUBLANES, SUBLANES, columns), axis=0)

    acc = lax.fori_loop(0, own_ref.shape[0] // TILE, body, jnp.zeros((SUBLANES, columns), F32))
    squares_ref[...] = jnp.sum(acc, axis=0, keepdims=True)


VMEM = pl.BlockSpec(memory_space=pltpu.VMEM)
SMEM = pl.BlockSpec(memory_space=pltpu.SMEM)
ANY = pl.BlockSpec(memory_space=pl.ANY)


def call(kernel, outs, in_specs, scratch=(), flops=0, limit=24):
    return pl.pallas_call(
        kernel,
        out_shape=[jax.ShapeDtypeStruct(s, d) for s, d in outs],
        in_specs=in_specs,
        out_specs=[VMEM] * len(outs),
        scratch_shapes=list(scratch),
        cost_estimate=pl.CostEstimate(flops=flops, bytes_accessed=8 << 20, transcendentals=0),
        compiler_params=pltpu.CompilerParams(vmem_limit_bytes=limit << 20),
    )


def local(factors, coupling, gap_loads, dof_blocks, partner_rows):
    subdomains, interface, columns = gap_loads.shape
    devices = lax.axis_size(SUB)
    position = lax.axis_index(SUB).astype(jnp.int32).reshape(1)
    rows = subdomains * interface
    slots = devices * FROWS
    place_flops = 2 * slots * rows * columns
    matrix_flops = 2 * slots * slots * columns

    def exchange(outgoing):
        blocks = outgoing.reshape(devices, FROWS, columns)
        incoming = lax.all_to_all(blocks, SUB, split_axis=0, concat_axis=0, tiled=True)
        return incoming.reshape(slots, columns)

    flat = gap_loads.reshape(rows, columns)
    gap, slot, order, sign = call(
        open_kernel,
        [
            ((slots, columns), BF16),
            ((1, rows), jnp.int32),
            ((rows // LANES, LANES), jnp.int32),
            ((rows // LANES, LANES), F32),
        ],
        [SMEM, ANY, ANY],
        [
            pltpu.VMEM(partner_rows.shape, jnp.int32),
            pltpu.VMEM((rows, columns), BF16),
            pltpu.VMEM((rows, LANES), F32),
            pltpu.SemaphoreType.DMA((2,)),
        ],
        flops=place_flops,
        limit=60,
    )(position, partner_rows, flat)
    incoming = exchange(gap)
    panels = jnp.stack(
        [whole_panel(factors[s], coupling[s], dof_blocks[s]) for s in range(subdomains)]
    )
    (matrix,) = call(
        build_kernel,
        [((slots, slots), BF16)],
        [VMEM] * 2,
        [pltpu.VMEM((slots, rows), BF16), pltpu.VMEM((TILE, rows), BF16)],
        flops=2 * slots * rows * slots,
        limit=28,
    )(slot, panels)
    column = jnp.broadcast_to(order.reshape(rows, 1), (rows, LANES))
    sign = jnp.broadcast_to(sign.reshape(rows, 1), (rows, LANES))
    state = ()
    for k in range(1, ITERS + 1):
        first, last = k == 1, k == ITERS
        outgoing, *following = call(
            functools.partial(step_kernel, first=first, last=last),
            [((slots, columns), BF16)] + [((slots, columns), F32)] * (not last),
            [VMEM] * (len(state) + 3),
            [pltpu.VMEM((slots, columns), BF16)],
            flops=matrix_flops,
            limit=20,
        )(*state, incoming, gap, matrix)
        arriving = exchange(outgoing)
        if last:
            own, multipliers = call(
                last_kernel,
                [((rows, columns), F32)] * 2,
                [VMEM] * 6,
                [pltpu.VMEM((slots, columns), BF16)] * 2,
                flops=3 * place_flops,
                limit=34,
            )(*state, incoming, flat, column, sign, panels)
        incoming, state = arriving, following
    residual, squares = call(
        close_kernel,
        [((rows, columns), F32), ((1, columns), F32)],
        [VMEM] * 4,
        flops=place_flops,
        limit=20,
    )(own, incoming, column, sign)
    for axes in (("sub_0",), ("sub_1", "sub_2")):
        copies = jnp.broadcast_to(squares[None], (lax.axis_size(axes),) + squares.shape)
        parts = lax.all_to_all(copies, axes, 0, 0, tiled=True)
        squares = jnp.sum(parts, axis=0)
    shape = (subdomains, interface, columns)
    return (
        multipliers.reshape(shape),
        residual.reshape(shape),
        jnp.sqrt(squares.reshape(columns) / (rows * devices) + 1e-06),
    )


def solution(mesh):
    finer = Mesh(
        mesh.devices.reshape(mesh.shape["grp"], 16, 4, 2), ("grp", "sub_0", "sub_1", "sub_2")
    )
    in_specs = (
        P(GRP_SUB, None, None),
        P(GRP_SUB, None, None),
        P(GRP_SUB, None, None),
        P(GRP_SUB),
        P(GRP_SUB, None),
    )
    out_specs = (P(GRP_SUB, None, None), P(GRP_SUB, None, None), P("grp"))
    return jax.shard_map(local, mesh=finer, in_specs=in_specs, out_specs=out_specs, check_vma=False)
```

time: 337 us -> 323 us (0.958)
  blocking collectives: 215 us -> 153 us
  waiting for transfers between devices: 29.4 us -> 45.7 us
  local copies, waits for them, and re-layouts: 5.21 us -> 18.1 us
  starting transfers between devices: 31.2 us -> 42.9 us
  Pallas kernels: 33.8 us -> 41.8 us
    all_to_all x3 -> x2, blocking collectives: 188 us -> 125 us  [exchange(): lax.all_to_all(blocks, SUB, split_axis=0, concat_axis=0, tiled=True)]
    all_to_all x1 -> x2, waiting for transfers between devices: 29.4 us -> 45.7 us  [exchange(): lax.all_to_all(blocks, SUB, split_axis=0, concat_axis=0, tiled=True)]
    unnamed x10 -> x32, local copies, waits for them, and re-layouts: 2.78 us -> 17 us
    all_to_all x1 -> x2, starting transfers between devices: 31.2 us -> 42.9 us  [exchange(): lax.all_to_all(blocks, SUB, split_axis=0, concat_axis=0, tiled=True)]
    pallas_call x5 -> x7, Pallas kernels: 33.8 us -> 41.8 us  [the longest x1 18 us: local(): call(build_kernel, [((slots, slots), BF16)], [VMEM] * 2, [pltpu.VMEM((slo...]
  transfers between devices with their start and end apart: 1 -> 2, of which waited for: 1 -> 2; matrix products, arithmetic and copies ran while one was open for 6% -> 6% of each run, Pallas kernels for 0% -> 7%
where the time goes in v2:
time: 323 us
  blocking collectives  153 us (47%)
  waiting for transfers between devices  45.7 us (14%)
  starting transfers between devices  42.9 us (13%)
  Pallas kernels  41.8 us (13%)
  local copies, waits for them, and re-layouts  18.1 us (6%)
  matrix products  17.9 us (6%)
    all_to_all x2, blocking collectives, exchange(): lax.all_to_all(blocks, SUB, split_axis=0, concat_axis=0, tiled=True)  125 us
    all_to_all x2, waiting for transfers between devices, exchange(): lax.all_to_all(blocks, SUB, split_axis=0, concat_axis=0, tiled=True)  45.7 us
    all_to_all x2, starting transfers between devices, exchange(): lax.all_to_all(blocks, SUB, split_axis=0, concat_axis=0, tiled=True)  42.9 us
    all_to_all x2, blocking collectives, local(): parts = lax.all_to_all(copies, axes, 0, 0, tiled=True)  27.4 us
    pallas_call x1, Pallas kernels, local(): call(build_kernel, [((slots, slots), BF16)], [VMEM] * 2, [pltpu.VMEM((slo...  18 us
    dot_general x3, matrix products, whole_panel(): lax.dot_general(reduced, reduced, (((0,), (0,)), ((), ())), preferred_ele...  17.9 us
    unnamed x32, local copies, waits for them, and re-layouts  17 us
    pallas_call x3, Pallas kernels, local(): call(functools.partial(step_kernel, first=first, last=last), [((slots, co...  8.5 us
  transfers between devices with their start and end apart: 2, of which 2 were waited for; matrix products, arithmetic and copies ran while one was open for 6% of the time, Pallas kernels for 7%

profile of v2, /device:TPU:33, one launch (start us, length us, event | category | flops | bytes accessed | tf_op | source)
XLA Modules:
  0.0 322.7 jit_solution(14937646188498310404)
XLA Ops:
  0.6 6.0 %shard_map.76 = (bf16[2048,256]{1,0:T(8,128)(2,1)}, s32[1,1536]{1,0:T(1,128)}, s32[12,128]{1,0:T(8,128)}, f32[12,128]{1,0:T(8,128)}) custom-call(s32[1]{0:T(128)} %bitcast.position_ref, s32[3,512]{1,0:T(4,128)} %partner_hbm.1, bf16[1536,256]{1,0:T(8,128)(2,1)} %bitcast.69), custom_call_target="tpu_custom_call" | custom-call | flops 1610612736 | bytes 8388608 | tf_op jit(solution)/shard_map/pallas_call | solution.py:244
  6.7 31.0 %all-to-all-start = ((bf16[128,16,256]{2,1,0:T(8,128)(2,1)}), bf16[128,16,256]{2,1,0:T(8,128)(2,1)S(1)}, u32[]{:S(2)}, u32[]{:S(2)}) async-start(bf16[128,16,256]{2,1,0:T(8,128)(2,1)} %bitcast.60), calls=%async_computation | async-start | bytes 2097152 | tf_op jit(solution)/shard_map/all_to_all | solution.py:240
  40.2 5.9 %fusion.15 = bf16[1,512,512]{2,1,0:T(8,128)(2,1)S(1)} fusion(bf16[3,1024,1024]{2,1,0:T(8,128)(2,1)} %param.5, bf16[3,1024,512]{2,1,0:T(8,128)(2,1)} %param.6, pred[1024]{0:T(1024)(128)(4,1)S(1)} %iota_compare_fusion.2), kind=kOutput, calls=%fused_computation.16 | convolution fusion | flops 1612447744 | bytes 3672064 | tf_op jit(solution)/shard_map/dot_general | solution.py:32
  46.1 5.9 %fusion.16 = bf16[1,512,512]{2,1,0:T(8,128)(2,1)S(1)} fusion(bf16[3,1024,1024]{2,1,0:T(8,128)(2,1)} %param.5, bf16[3,1024,512]{2,1,0:T(8,128)(2,1)} %param.6, pred[1024]{0:T(1024)(128)(4,1)S(1)} %iota_compare_fusion.1), kind=kOutput, calls=%fused_computation.17 | convolution fusion | flops 1612447744 | bytes 3672064 | tf_op jit(solution)/shard_map/dot_general | solution.py:32
  52.0 6.2 %fusion.17 = bf16[1,512,512]{2,1,0:T(8,128)(2,1)S(1)} fusion(bf16[3,1024,1024]{2,1,0:T(8,128)(2,1)} %param.5, bf16[3,1024,512]{2,1,0:T(8,128)(2,1)} %param.6, pred[1024]{0:T(1024)(128)(4,1)S(1)} %iota_compare_fusion), kind=kOutput, calls=%fused_computation.18 | convolution fusion | flops 1612447744 | bytes 3672064 | tf_op jit(solution)/shard_map/dot_general | solution.py:32
  58.9 18.0 %shard_map.77.refs_2_.refs_3_ = bf16[2048,2048]{1,0:T(8,128)(2,1)S(1)} custom-call(s32[1,1536]{1,0:T(1,128)S(1)} %copy-done.12, bf16[3,512,512]{2,1,0:T(8,128)(2,1)S(1)} %pad_maximum_fusion.panel_ref), custom_call_target="tpu_custom_call" | custom-call | flops 12884901888 | bytes 8388608 | tf_op jit(solution)/shard_map/pallas_call | solution.py:266
  76.9 3.2 copy-done
  80.1 1.1 copy-done.5
  81.3 7.4 %all-to-all-done = bf16[128,16,256]{2,1,0:T(8,128)(2,1)S(1)} async-done(((bf16[128,16,256]{2,1,0:T(8,128)(2,1)}), bf16[128,16,256]{2,1,0:T(8,128)(2,1)S(1)}, u32[]{:S(2)}, u32[]{:S(2)}) %all-to-all-start) | async-done | bytes 1048608 | tf_op jit(solution)/shard_map/all_to_all | solution.py:240
  88.7 3.4 %copy-done.1 = bf16[2048,2048]{1,0:T(8,128)(2,1)S(1)} copy-done((bf16[2048,2048]{1,0:T(8,128)(2,1)S(1)}, bf16[2048,2048]{1,0:T(8,128)(2,1)}, u32[]{:S(2)}) %copy-start.1) | copy-done | bytes 8388632
  92.1 2.6 shard_map.78
  94.7 62.8 %all_to_all.30 = bf16[128,16,256]{2,1,0:T(8,128)(2,1)S(1)} all-to-all(bf16[128,16,256]{2,1,0:T(8,128)(2,1)S(1)} %bitcast.67), channel_id=1, replica_groups=mesh['grp'=2,'sub_0'=16,'sub_1'=4,'sub_2'=2] {'sub_0','sub_1','sub_2'}, dimensions={0} | all-to-all | bytes 2097152 | tf_op jit(solution)/shard_map/all_to_all | solution.py:240
  157.4 2.6 shard_map.79
  160.0 62.5 %all_to_all.31 = bf16[128,16,256]{2,1,0:T(8,128)(2,1)S(1)} all-to-all(bf16[128,16,256]{2,1,0:T(8,128)(2,1)S(1)} %bitcast.66), channel_id=1, replica_groups=mesh['grp'=2,'sub_0'=16,'sub_1'=4,'sub_2'=2] {'sub_0','sub_1','sub_2'}, dimensions={0} | all-to-all | bytes 2097152 | tf_op jit(solution)/shard_map/all_to_all | solution.py:240
  222.6 3.3 %shard_map.81 = bf16[2048,256]{1,0:T(8,128)(2,1)} custom-call(f32[2048,256]{1,0:T(8,128)S(1)} %get-tuple-element.19.base_ref.refs_0_, bf16[2048,256]{1,0:T(8,128)(2,1)S(1)} %bitcast.63, bf16[2048,256]{1,0:T(8,128)(2,1)S(1)} %copy-done.2, bf16[2048,2048]{1,0:T(8,128)(2,1)S(1)} %copy-done.1), custom_call_target="tpu_custom_call" | custom-call | flops 2147483648 | bytes 8388608 | tf_op jit(solution)/shard_map/pallas_call | solution.py:279
  225.9 11.9 %all-to-all-start.3 = ((bf16[128,16,256]{2,1,0:T(8,128)(2,1)}), bf16[128,16,256]{2,1,0:T(8,128)(2,1)S(1)}, u32[]{:S(2)}, u32[]{:S(2)}) async-start(bf16[128,16,256]{2,1,0:T(8,128)(2,1)} %bitcast.23), calls=%async_computation.3 | async-start | bytes 2097152 | tf_op jit(solution)/shard_map/all_to_all | solution.py:240
  238.3 1.6 copy-done.4
  239.9 1.4 copy-done.6
  242.5 5.9 %shard_map.80 = (f32[1536,256]{1,0:T(8,128)S(1)}, f32[1536,256]{1,0:T(8,128)}) custom-call(f32[2048,256]{1,0:T(8,128)S(1)} %copy-done.4, bf16[2048,256]{1,0:T(8,128)(2,1)S(1)} %bitcast.64, bf16[1536,256]{1,0:T(8,128)(2,1)S(1)} %bitcast.70, s32[1536,128]{1,0:T(8,128)S(1)} %broadcast_in_dim.77.column_ref, f32[1536,128]{1,0:T(8,128)S(1)} %broadcast_in_dim.79.sign_ref, ...), custom_call_target="tpu_custom_call" | custom-call | flops 4831838208 | bytes 8388608 | tf_op jit(solution)/shard_map/pallas_call | solution.py:289
  250.4 38.3 %all-to-all-done.3 = bf16[128,16,256]{2,1,0:T(8,128)(2,1)S(1)} async-done(((bf16[128,16,256]{2,1,0:T(8,128)(2,1)}), bf16[128,16,256]{2,1,0:T(8,128)(2,1)S(1)}, u32[]{:S(2)}, u32[]{:S(2)}) %all-to-all-start.3) | async-done | bytes 1048608 | tf_op jit(solution)/shard_map/all_to_all | solution.py:240
  289.9 1.4 copy-done.11
  291.3 3.3 %shard_map.82 = (f32[1536,256]{1,0:T(8,128)}, f32[1,256]{1,0:T(1,128)S(1)}) custom-call(f32[1536,256]{1,0:T(8,128)S(1)} %copy-done.11, bf16[2048,256]{1,0:T(8,128)(2,1)S(1)} %bitcast.65, s32[1536,128]{1,0:T(8,128)S(1)} %broadcast_in_dim.77.column_ref, f32[1536,128]{1,0:T(8,128)S(1)} %copy-done.8), custom_call_target="tpu_custom_call" | custom-call | flops 1610612736 | bytes 8388608 | tf_op jit(solution)/shard_map/pallas_call | solution.py:298
  294.6 18.5 %all_to_all.32 = f32[16,1,256]{2,1,0:T(1,128)S(1)} all-to-all(f32[16,1,256]{2,1,0:T(1,128)S(1)} %broadcast_in_dim.81), channel_id=1, replica_groups=mesh['grp'=2,'sub_0'=16,'sub_1'=4,'sub_2'=2] {'sub_0'}, dimensions={0} | all-to-all | bytes 32768 | tf_op jit(solution)/shard_map/all_to_all | solution.py:307
  313.2 8.9 %all_to_all.33 = f32[8,1,256]{2,1,0:T(1,128)S(1)} all-to-all(f32[8,1,256]{2,1,0:T(1,128)S(1)} %broadcast_in_dim.82), channel_id=1, replica_groups=mesh['grp'=2,'sub_0'=16,'sub_1'=4,'sub_2'=2] {'sub_1','sub_2'}, dimensions={0} | all-to-all | bytes 16384 | tf_op jit(solution)/shard_map/all_to_all | solution.py:307
  (38 shorter events, 6.8 us)
Async XLA Ops:
  6.7 31.1 %copy-start.15 = (s32[3]{0:T(128)S(1)}, s32[3]{0:T(128)}, u32[]{:S(2)}) copy-start(s32[3]{0:T(128)} %param.8) | copy-start | bytes 40
  6.7 82.0 %all-to-all-start = ((bf16[128,16,256]{2,1,0:T(8,128)(2,1)}), bf16[128,16,256]{2,1,0:T(8,128)(2,1)S(1)}, u32[]{:S(2)}, u32[]{:S(2)}) async-start(bf16[128,16,256]{2,1,0:T(8,128)(2,1)} %bitcast.60), calls=%async_computation | async-start | bytes 2097152 | tf_op jit(solution)/shard_map/all_to_all | solution.py:240
  58.2 0.7 copy-start.12
  58.9 29.8 %copy-start.2 = (bf16[2048,256]{1,0:T(8,128)(2,1)S(1)}, bf16[2048,256]{1,0:T(8,128)(2,1)}, u32[]{:S(2)}) copy-start(bf16[2048,256]{1,0:T(8,128)(2,1)} %get-tuple-element.15.refs_1_.refs_2_) | copy-start | bytes 3145732
  76.9 3.2 %copy-start = (bf16[2048,2048]{1,0:T(8,128)(2,1)}, bf16[2048,2048]{1,0:T(8,128)(2,1)S(1)}, u32[]{:S(2)}) copy-start(bf16[2048,2048]{1,0:T(8,128)(2,1)S(1)} %shard_map.77.refs_2_.refs_3_) | copy-start | bytes 25165828
  80.1 1.1 copy-start.5
  88.7 3.4 %copy-start.1 = (bf16[2048,2048]{1,0:T(8,128)(2,1)S(1)}, bf16[2048,2048]{1,0:T(8,128)(2,1)}, u32[]{:S(2)}) copy-start(bf16[2048,2048]{1,0:T(8,128)(2,1)} %copy-done) | copy-start | bytes 25165828
  160.0 65.9 %copy-start.3 = (f32[2048,256]{1,0:T(8,128)}, f32[2048,256]{1,0:T(8,128)S(1)}, u32[]{:S(2)}) copy-start(f32[2048,256]{1,0:T(8,128)S(1)} %get-tuple-element.19.base_ref.refs_0_) | copy-start | bytes 6291460
  225.9 11.9 %copy-start.14 = (s32[12,128]{1,0:T(8,128)S(1)}, s32[12,128]{1,0:T(8,128)}, u32[]{:S(2)}) copy-start(s32[12,128]{1,0:T(8,128)} %get-tuple-element.21) | copy-start | bytes 18436
  225.9 12.2 %copy-start.13 = (f32[12,128]{1,0:T(8,128)S(1)}, f32[12,128]{1,0:T(8,128)}, u32[]{:S(2)}) copy-start(f32[12,128]{1,0:T(8,128)} %get-tuple-element.22) | copy-start | bytes 18436
  225.9 62.9 %all-to-all-start.3 = ((bf16[128,16,256]{2,1,0:T(8,128)(2,1)}), bf16[128,16,256]{2,1,0:T(8,128)(2,1)S(1)}, u32[]{:S(2)}, u32[]{:S(2)}) async-start(bf16[128,16,256]{2,1,0:T(8,128)(2,1)} %bitcast.23), calls=%async_computation.3 | async-start | bytes 2097152 | tf_op jit(solution)/shard_map/all_to_all | solution.py:240
  238.3 1.6 copy-start.4
  239.9 1.4 copy-start.6
  241.3 1.1 copy-start.9
  248.4 0.9 copy-start.7
  249.3 1.1 copy-start.10
  288.8 1.1 copy-start.8
  289.9 1.4 copy-start.11

commit v3 on v2

--- a/solution.py
+++ b/solution.py
@@ -40,7 +40,7 @@
     return jnp.where(ids == slot_ref[...], 1.0, 0.0).astype(BF16)
 
 
-def open_kernel(position_ref, partner_hbm, gap_hbm, send_ref, slot_ref, order_ref, sign_ref, partner_ref, gap_ref, comp, sems):
+def open_kernel(position_ref, partner_hbm, gap_hbm, send_ref, slot_ref, order_ref, partner_ref, gap_ref, comp, sems):
     load_partner = pltpu.make_async_copy(partner_hbm, partner_ref, sems.at[0])
     load_gap = pltpu.make_async_copy(gap_hbm, gap_ref, sems.at[1])
     load_partner.start()
@@ -65,9 +65,7 @@
         + lax.broadcasted_iota(jnp.int32, (tiles, LANES), 1)
     ).astype(F32)
     first = target * span
-    lower = position_ref[0].astype(F32) < target
-    sign_ref[...] = jnp.where(lower, 1.0, -1.0)
-    full = first + jnp.where(lower, ordinal, remote)
+    full = first + jnp.where(position_ref[0].astype(F32) < target, ordinal, remote)
     for t in range(tiles):
         comp[t * LANES : (t + 1) * LANES, :] = jnp.broadcast_to(
             full[t : t + 1, :], (LANES, LANES)
@@ -160,11 +158,12 @@
     return jnp.concatenate(pieces, axis=1)
 
 
-def across(sign_ref, here, columns):
-    return jnp.concatenate([sign_ref[here, :]] * (columns // LANES), axis=1)
-
-
-def last_kernel(base_ref, incoming_ref, gap_ref, column_ref, sign_ref, panel_ref,
+def orient(position_ref, column_ref, here, columns):
+    after = column_ref[here, :] >= (position_ref[0] + 1) * FROWS
+    return jnp.concatenate([jnp.where(after, 1.0, -1.0)] * (columns // LANES), axis=1)
+
+
+def last_kernel(position_ref, base_ref, incoming_ref, gap_ref, column_ref, panel_ref,
                 own_ref, mult_ref, signed, low):
     slots, columns = signed.shape
 
@@ -184,7 +183,7 @@
         chosen = chosen_slots(column_ref, base, slots)
         high = jnp.dot(chosen, signed[...], preferred_element_type=F32)
         rest = jnp.dot(chosen, low[...], preferred_element_type=F32)
-        mult_ref[here, :] = across(sign_ref, here, columns) * (high + rest)
+        mult_ref[here, :] = orient(position_ref, column_ref, here, columns) * (high + rest)
         image = jnp.dot(panel_ref[s], high.astype(BF16), preferred_element_type=F32)
         own_ref[here, :] = gap_ref[here, :].astype(F32) - image
         return carry
@@ -192,7 +191,7 @@
     lax.fori_loop(0, panel_ref.shape[0], rows, 0)
 
 
-def close_kernel(own_ref, incoming_ref, column_ref, sign_ref, residual_ref, squares_ref):
+def close_kernel(position_ref, own_ref, incoming_ref, column_ref, residual_ref, squares_ref):
     slots, columns = incoming_ref.shape
 
     def body(s, acc):
@@ -202,7 +201,7 @@
             chosen_slots(column_ref, base, slots), incoming_ref[...], preferred_element_type=F32
         )
         residual = own_ref[here, :] - landed
-        residual_ref[here, :] = across(sign_ref, here, columns) * residual
+        residual_ref[here, :] = orient(position_ref, column_ref, here, columns) * residual
         return acc + jnp.sum((residual * residual).reshape(TILE // SUBLANES, SUBLANES, columns), axis=0)
 
     acc = lax.fori_loop(0, own_ref.shape[0] // TILE, body, jnp.zeros((SUBLANES, columns), F32))
@@ -241,13 +240,12 @@
         return incoming.reshape(slots, columns)
 
     flat = gap_loads.reshape(rows, columns)
-    gap, slot, order, sign = call(
+    gap, slot, order = call(
         open_kernel,
         [
             ((slots, columns), BF16),
             ((1, rows), jnp.int32),
             ((rows // LANES, LANES), jnp.int32),
-            ((rows // LANES, LANES), F32),
         ],
         [SMEM, ANY, ANY],
         [
@@ -272,7 +270,6 @@
         limit=28,
     )(slot, panels)
     column = jnp.broadcast_to(order.reshape(rows, 1), (rows, LANES))
-    sign = jnp.broadcast_to(sign.reshape(rows, 1), (rows, LANES))
     state = ()
     for k in range(1, ITERS + 1):
         first, last = k == 1, k == ITERS
@@ -289,19 +286,19 @@
             own, multipliers = call(
                 last_kernel,
                 [((rows, columns), F32)] * 2,
-                [VMEM] * 6,
+                [SMEM] + [VMEM] * 5,
                 [pltpu.VMEM((slots, columns), BF16)] * 2,
                 flops=3 * place_flops,
                 limit=34,
-            )(*state, incoming, flat, column, sign, panels)
+            )(position, *state, incoming, flat, column, panels)
         incoming, state = arriving, following
     residual, squares = call(
         close_kernel,
         [((rows, columns), F32), ((1, columns), F32)],
-        [VMEM] * 4,
+        [SMEM] + [VMEM] * 3,
         flops=place_flops,
         limit=20,
-    )(own, incoming, column, sign)
+    )(position, own, incoming, column)
     for axes in (("sub_0",), ("sub_1", "sub_2")):
         copies = jnp.broadcast_to(squares[None], (lax.axis_size(axes),) + squares.shape)
         parts = lax.all_to_all(copies, axes, 0, 0, tiled=True)

time: 323 us -> 322 us (level)
    unnamed x32 -> x26, local copies, waits for them, and re-layouts: 17 us -> 14.9 us
where the time goes in v3:
time: 322 us
  blocking collectives  153 us (48%)
  waiting for transfers between devices  46.9 us (15%)
  starting transfers between devices  42.9 us (13%)
  Pallas kernels  41.8 us (13%)
  matrix products  17.9 us (6%)
  local copies, waits for them, and re-layouts  15.9 us (5%)
    all_to_all x2, blocking collectives, exchange(): lax.all_to_all(blocks, SUB, split_axis=0, concat_axis=0, tiled=True)  125 us
    all_to_all x2, waiting for transfers between devices, exchange(): lax.all_to_all(blocks, SUB, split_axis=0, concat_axis=0, tiled=True)  46.9 us
    all_to_all x2, starting transfers between devices, exchange(): lax.all_to_all(blocks, SUB, split_axis=0, concat_axis=0, tiled=True)  42.9 us
    all_to_all x2, blocking collectives, local(): parts = lax.all_to_all(copies, axes, 0, 0, tiled=True)  27.4 us
    pallas_call x1, Pallas kernels, local(): call(build_kernel, [((slots, slots), BF16)], [VMEM] * 2, [pltpu.VMEM((slo...  18 us
    dot_general x3, matrix products, whole_panel(): lax.dot_general(reduced, reduced, (((0,), (0,)), ((), ())), preferred_ele...  17.9 us
    unnamed x26, local copies, waits for them, and re-layouts  14.9 us
    pallas_call x3, Pallas kernels, local(): call(functools.partial(step_kernel, first=first, last=last), [((slots, co...  8.48 us
  transfers between devices with their start and end apart: 2, of which 2 were waited for; matrix products, arithmetic and copies ran while one was open for 6% of the time, Pallas kernels for 7%

profile of v3, /device:TPU:33, one launch (start us, length us, event | category | flops | bytes accessed | tf_op | source)
XLA Modules:
  0.0 321.5 jit_solution(17553140143046249548)
XLA Ops:
  0.6 6.0 %shard_map.76 = (bf16[2048,256]{1,0:T(8,128)(2,1)}, s32[1,1536]{1,0:T(1,128)}, s32[12,128]{1,0:T(8,128)}) custom-call(s32[1]{0:T(128)} %bitcast.position_ref, s32[3,512]{1,0:T(4,128)} %partner_hbm.1, bf16[1536,256]{1,0:T(8,128)(2,1)} %bitcast.68), custom_call_target="tpu_custom_call" | custom-call | flops 1610612736 | bytes 8388608 | tf_op jit(solution)/shard_map/pallas_call | solution.py:243
  6.7 31.0 %all-to-all-start = ((bf16[128,16,256]{2,1,0:T(8,128)(2,1)}), bf16[128,16,256]{2,1,0:T(8,128)(2,1)S(1)}, u32[]{:S(2)}, u32[]{:S(2)}) async-start(bf16[128,16,256]{2,1,0:T(8,128)(2,1)} %bitcast.59), calls=%async_computation | async-start | bytes 2097152 | tf_op jit(solution)/shard_map/all_to_all | solution.py:239
  40.2 5.9 %fusion.15 = bf16[1,512,512]{2,1,0:T(8,128)(2,1)S(1)} fusion(bf16[3,1024,1024]{2,1,0:T(8,128)(2,1)} %param.5, bf16[3,1024,512]{2,1,0:T(8,128)(2,1)} %param.6, pred[1024]{0:T(1024)(128)(4,1)S(1)} %iota_compare_fusion.2), kind=kOutput, calls=%fused_computation.16 | convolution fusion | flops 1612447744 | bytes 3672064 | tf_op jit(solution)/shard_map/dot_general | solution.py:32
  46.2 5.9 %fusion.16 = bf16[1,512,512]{2,1,0:T(8,128)(2,1)S(1)} fusion(bf16[3,1024,1024]{2,1,0:T(8,128)(2,1)} %param.5, bf16[3,1024,512]{2,1,0:T(8,128)(2,1)} %param.6, pred[1024]{0:T(1024)(128)(4,1)S(1)} %iota_compare_fusion.1), kind=kOutput, calls=%fused_computation.17 | convolution fusion | flops 1612447744 | bytes 3672064 | tf_op jit(solution)/shard_map/dot_general | solution.py:32
  52.0 6.2 %fusion.17 = bf16[1,512,512]{2,1,0:T(8,128)(2,1)S(1)} fusion(bf16[3,1024,1024]{2,1,0:T(8,128)(2,1)} %param.5, bf16[3,1024,512]{2,1,0:T(8,128)(2,1)} %param.6, pred[1024]{0:T(1024)(128)(4,1)S(1)} %iota_compare_fusion), kind=kOutput, calls=%fused_computation.18 | convolution fusion | flops 1612447744 | bytes 3672064 | tf_op jit(solution)/shard_map/dot_general | solution.py:32
  58.9 18.0 %shard_map.77.refs_2_.refs_3_ = bf16[2048,2048]{1,0:T(8,128)(2,1)S(1)} custom-call(s32[1,1536]{1,0:T(1,128)S(1)} %copy-done.10, bf16[3,512,512]{2,1,0:T(8,128)(2,1)S(1)} %pad_maximum_fusion.panel_ref), custom_call_target="tpu_custom_call" | custom-call | flops 12884901888 | bytes 8388608 | tf_op jit(solution)/shard_map/pallas_call | solution.py:264
  76.9 3.2 %copy-done = bf16[2048,2048]{1,0:T(8,128)(2,1)} copy-done((bf16[2048,2048]{1,0:T(8,128)(2,1)}, bf16[2048,2048]{1,0:T(8,128)(2,1)S(1)}, u32[]{:S(2)}) %copy-start) | copy-done | bytes 8388632
  80.2 1.1 copy-done.5
  81.3 7.4 %all-to-all-done = bf16[128,16,256]{2,1,0:T(8,128)(2,1)S(1)} async-done(((bf16[128,16,256]{2,1,0:T(8,128)(2,1)}), bf16[128,16,256]{2,1,0:T(8,128)(2,1)S(1)}, u32[]{:S(2)}, u32[]{:S(2)}) %all-to-all-start) | async-done | bytes 1048608 | tf_op jit(solution)/shard_map/all_to_all | solution.py:239
  88.7 3.4 %copy-done.1 = bf16[2048,2048]{1,0:T(8,128)(2,1)S(1)} copy-done((bf16[2048,2048]{1,0:T(8,128)(2,1)S(1)}, bf16[2048,2048]{1,0:T(8,128)(2,1)}, u32[]{:S(2)}) %copy-start.1) | copy-done | bytes 8388632
  92.1 2.6 shard_map.78
  94.7 62.8 %all_to_all.30 = bf16[128,16,256]{2,1,0:T(8,128)(2,1)S(1)} all-to-all(bf16[128,16,256]{2,1,0:T(8,128)(2,1)S(1)} %bitcast.66), channel_id=1, replica_groups=mesh['grp'=2,'sub_0'=16,'sub_1'=4,'sub_2'=2] {'sub_0','sub_1','sub_2'}, dimensions={0} | all-to-all | bytes 2097152 | tf_op jit(solution)/shard_map/all_to_all | solution.py:239
  157.4 2.6 shard_map.79
  160.0 62.5 %all_to_all.31 = bf16[128,16,256]{2,1,0:T(8,128)(2,1)S(1)} all-to-all(bf16[128,16,256]{2,1,0:T(8,128)(2,1)S(1)} %bitcast.65), channel_id=1, replica_groups=mesh['grp'=2,'sub_0'=16,'sub_1'=4,'sub_2'=2] {'sub_0','sub_1','sub_2'}, dimensions={0} | all-to-all | bytes 2097152 | tf_op jit(solution)/shard_map/all_to_all | solution.py:239
  222.6 3.3 %shard_map.81 = bf16[2048,256]{1,0:T(8,128)(2,1)} custom-call(f32[2048,256]{1,0:T(8,128)S(1)} %get-tuple-element.18.base_ref.refs_0_, bf16[2048,256]{1,0:T(8,128)(2,1)S(1)} %bitcast.62, bf16[2048,256]{1,0:T(8,128)(2,1)S(1)} %copy-done.2, bf16[2048,2048]{1,0:T(8,128)(2,1)S(1)} %copy-done.1), custom_call_target="tpu_custom_call" | custom-call | flops 2147483648 | bytes 8388608 | tf_op jit(solution)/shard_map/pallas_call | solution.py:276
  225.9 11.9 %all-to-all-start.3 = ((bf16[128,16,256]{2,1,0:T(8,128)(2,1)}), bf16[128,16,256]{2,1,0:T(8,128)(2,1)S(1)}, u32[]{:S(2)}, u32[]{:S(2)}) async-start(bf16[128,16,256]{2,1,0:T(8,128)(2,1)} %bitcast.22), calls=%async_computation.3 | async-start | bytes 2097152 | tf_op jit(solution)/shard_map/all_to_all | solution.py:239
  238.0 1.6 copy-done.4
  239.6 1.4 copy-done.6
  242.2 5.9 %shard_map.80 = (f32[1536,256]{1,0:T(8,128)S(1)}, f32[1536,256]{1,0:T(8,128)}) custom-call(s32[1]{0:T(128)} %bitcast.position_ref, f32[2048,256]{1,0:T(8,128)S(1)} %copy-done.4, bf16[2048,256]{1,0:T(8,128)(2,1)S(1)} %bitcast.63, bf16[1536,256]{1,0:T(8,128)(2,1)S(1)} %bitcast.69, s32[1536,128]{1,0:T(8,128)S(1)} %broadcast_in_dim.70.column_ref, ...), custom_call_target="tpu_custom_call" | custom-call | flops 4831838208 | bytes 8388608 | tf_op jit(solution)/shard_map/pallas_call | solution.py:286
  249.2 39.5 %all-to-all-done.3 = bf16[128,16,256]{2,1,0:T(8,128)(2,1)S(1)} async-done(((bf16[128,16,256]{2,1,0:T(8,128)(2,1)}), bf16[128,16,256]{2,1,0:T(8,128)(2,1)S(1)}, u32[]{:S(2)}, u32[]{:S(2)}) %all-to-all-start.3) | async-done | bytes 1048608 | tf_op jit(solution)/shard_map/all_to_all | solution.py:239
  288.7 1.4 copy-done.9
  290.1 3.3 %shard_map.82 = (f32[1536,256]{1,0:T(8,128)}, f32[1,256]{1,0:T(1,128)S(1)}) custom-call(s32[1]{0:T(128)} %bitcast.position_ref, f32[1536,256]{1,0:T(8,128)S(1)} %copy-done.9, bf16[2048,256]{1,0:T(8,128)(2,1)S(1)} %bitcast.64, s32[1536,128]{1,0:T(8,128)S(1)} %broadcast_in_dim.70.column_ref), custom_call_target="tpu_custom_call" | custom-call | flops 1610612736 | bytes 8388608 | tf_op jit(solution)/shard_map/pallas_call | solution.py:295
  293.5 18.5 %all_to_all.32 = f32[16,1,256]{2,1,0:T(1,128)S(1)} all-to-all(f32[16,1,256]{2,1,0:T(1,128)S(1)} %broadcast_in_dim.72), channel_id=1, replica_groups=mesh['grp'=2,'sub_0'=16,'sub_1'=4,'sub_2'=2] {'sub_0'}, dimensions={0} | all-to-all | bytes 32768 | tf_op jit(solution)/shard_map/all_to_all | solution.py:304
  312.0 8.9 %all_to_all.33 = f32[8,1,256]{2,1,0:T(1,128)S(1)} all-to-all(f32[8,1,256]{2,1,0:T(1,128)S(1)} %broadcast_in_dim.73), channel_id=1, replica_groups=mesh['grp'=2,'sub_0'=16,'sub_1'=4,'sub_2'=2] {'sub_1','sub_2'}, dimensions={0} | all-to-all | bytes 16384 | tf_op jit(solution)/shard_map/all_to_all | solution.py:304
  (31 shorter events, 4.6 us)
Async XLA Ops:
  6.7 31.1 %copy-start.12 = (s32[3]{0:T(128)S(1)}, s32[3]{0:T(128)}, u32[]{:S(2)}) copy-start(s32[3]{0:T(128)} %param.8) | copy-start | bytes 40
  6.7 82.0 %all-to-all-start = ((bf16[128,16,256]{2,1,0:T(8,128)(2,1)}), bf16[128,16,256]{2,1,0:T(8,128)(2,1)S(1)}, u32[]{:S(2)}, u32[]{:S(2)}) async-start(bf16[128,16,256]{2,1,0:T(8,128)(2,1)} %bitcast.59), calls=%async_computation | async-start | bytes 2097152 | tf_op jit(solution)/shard_map/all_to_all | solution.py:239
  58.2 0.7 copy-start.10
  58.9 29.8 %copy-start.2 = (bf16[2048,256]{1,0:T(8,128)(2,1)S(1)}, bf16[2048,256]{1,0:T(8,128)(2,1)}, u32[]{:S(2)}) copy-start(bf16[2048,256]{1,0:T(8,128)(2,1)} %get-tuple-element.14.refs_1_.refs_2_) | copy-start | bytes 3145732
  76.9 3.2 %copy-start = (bf16[2048,2048]{1,0:T(8,128)(2,1)}, bf16[2048,2048]{1,0:T(8,128)(2,1)S(1)}, u32[]{:S(2)}) copy-start(bf16[2048,2048]{1,0:T(8,128)(2,1)S(1)} %shard_map.77.refs_2_.refs_3_) | copy-start | bytes 25165828
  80.2 1.1 copy-start.5
  88.7 3.4 %copy-start.1 = (bf16[2048,2048]{1,0:T(8,128)(2,1)S(1)}, bf16[2048,2048]{1,0:T(8,128)(2,1)}, u32[]{:S(2)}) copy-start(bf16[2048,2048]{1,0:T(8,128)(2,1)} %copy-done) | copy-start | bytes 25165828
  160.0 65.8 %copy-start.3 = (f32[2048,256]{1,0:T(8,128)}, f32[2048,256]{1,0:T(8,128)S(1)}, u32[]{:S(2)}) copy-start(f32[2048,256]{1,0:T(8,128)S(1)} %get-tuple-element.18.base_ref.refs_0_) | copy-start | bytes 6291460
  225.9 11.9 %copy-start.11 = (s32[12,128]{1,0:T(8,128)S(1)}, s32[12,128]{1,0:T(8,128)}, u32[]{:S(2)}) copy-start(s32[12,128]{1,0:T(8,128)} %get-tuple-element.20) | copy-start | bytes 18436
  225.9 62.9 %all-to-all-start.3 = ((bf16[128,16,256]{2,1,0:T(8,128)(2,1)}), bf16[128,16,256]{2,1,0:T(8,128)(2,1)S(1)}, u32[]{:S(2)}, u32[]{:S(2)}) async-start(bf16[128,16,256]{2,1,0:T(8,128)(2,1)} %bitcast.22), calls=%async_computation.3 | async-start | bytes 2097152 | tf_op jit(solution)/shard_map/all_to_all | solution.py:239
  238.0 1.6 copy-start.4
  239.6 1.4 copy-start.6
  241.0 1.1 copy-start.7
  248.1 1.1 copy-start.8
  288.7 1.4 copy-start.9
